TPU v7x, 32 devices: a whole 2x2x4 slice. The times are simulated.
32 devices in a mesh: dp: 8 (over z, x), mp: 4 (over y, core).
Axes of the slice: x: 2, y: 2, z: 4, core: 2. Of those that a mesh axis runs over, the one named last changes fastest.
Arguments:
- hidden_in: bfloat16 [2, 1024, 3584], P(None, 'dp', 'mp'), may hold values from -6 to 6
- out_grad: bfloat16 [2, 1024, 3584], P(None, 'dp', 'mp'), may hold values from -1536 to 1536
- pack_fill: int32 [2, 8], P(None, 'dp'), may hold values from 1 to 128, as said below
- norm_gain: float32 [3584], P('mp'), may hold values from 0.5 to 1.5
- up_weight: bfloat16 [3584, 7168], P(None, 'mp'), may hold values from -0.09375 to 0.09375
- down_weight: bfloat16 [7168, 3584], P('mp'), may hold values from -0.0625 to 0.0625
Outputs:
- in_grad: bfloat16 [2, 1024, 3584], P(None, 'dp', 'mp')
- up_grad: float32 [3584, 7168], P('dp', 'mp')
- down_grad: float32 [7168, 3584], P('mp', 'dp')
- gain_grad: float32 [3584], P('mp')
Inputs may be any that keep to these rules, and one draw needn't show every extreme that they name: pack_fill[m, p] real tokens stand at the start of pack p of microbatch m (positions p * 128 onward); the other positions of the pack are padding and carry no loss. In every draw the last pack of the first microbatch is full.
All inputs are finite; a program needn't handle non-finite values.
Results may differ from a plain program's by a relative error of at most 0.014.
Values may be sent and summed in bfloat16 or wider, within the bound.
A program may use at most 128 MiB of HBM per device.

v0:
```python
import jax
import jax.numpy as jnp
from jax import lax
from jax.sharding import PartitionSpec as P

TOK_DEV = 128
MICRO = 2
BLOCK = 128


epsilon = 1e-06


def gelu_tanh(value):
    return jax.nn.gelu(value, approximate=True)


def contract_rows(left, right):
    return lax.dot_general(
        left, right, (((0,), (0,)), ((), ())), preferred_element_type=jnp.float32
    )


def contract_cols(left, right):
    return lax.dot_general(
        left, right, (((1,), (1,)), ((), ())), preferred_element_type=jnp.float32
    )


def block_grads(tok_rows, grad_rows, live_mask, inv_count, weights):
    norm_gain, up_weight, down_weight = weights
    model_width = up_weight.shape[0]
    values = tok_rows.astype(jnp.float32)
    squares = lax.psum(jnp.sum(values * values, axis=1), "mp")
    inv_rms = lax.rsqrt(squares / model_width + epsilon)[:, None]
    normed = (values * inv_rms * norm_gain[None, :]).astype(jnp.bfloat16)
    scaled = (grad_rows.astype(jnp.float32) * live_mask[:, None] * inv_count).astype(jnp.bfloat16)
    normed_full, scaled_full = (
        lax.all_gather(normed, "mp", axis=1, tiled=True),
        lax.all_gather(scaled, "mp", axis=1, tiled=True),
    )
    pre_act = jnp.dot(normed_full, up_weight, preferred_element_type=jnp.float32)
    activated = gelu_tanh(pre_act).astype(jnp.bfloat16)
    grad_act = contract_cols(scaled_full, down_weight)
    grad_pre = jax.vjp(gelu_tanh, pre_act)[1](grad_act)[0].astype(jnp.bfloat16)
    grad_normed = lax.psum_scatter(
        contract_cols(grad_pre, up_weight).astype(jnp.bfloat16),
        "mp",
        scatter_dimension=1,
        tiled=True,
    ).astype(jnp.float32)
    row_dot = lax.psum(jnp.sum(grad_normed * norm_gain[None, :] * values, axis=1), "mp")[:, None]
    cubed = inv_rms * inv_rms * inv_rms
    in_rows = (
        scaled.astype(jnp.float32)
        + norm_gain[None, :] * grad_normed * inv_rms
        - values * cubed * row_dot / model_width
    )
    gain_term = jnp.sum(grad_normed * values * inv_rms, axis=0)
    return (in_rows.astype(jnp.bfloat16), normed_full, grad_pre, activated, scaled_full, gain_term)


def run_rows(tok_rows, grad_rows, live_count, count_blocks, inv_count, weights, carried, row_base):
    out_rows = jnp.zeros(tok_rows.shape, jnp.bfloat16)

    def block_step(block_index, current):
        out_rows, down_acc, gain_acc, kept_terms = current
        row_start = block_index * BLOCK
        live_mask = (row_start + jnp.arange(BLOCK, dtype=jnp.int32) < live_count).astype(
            jnp.float32
        )
        in_rows, normed_full, grad_pre, activated, scaled_full, gain_term = block_grads(
            tok_rows, grad_rows, live_mask, inv_count, weights
        )
        out_rows = in_rows
        down_acc = down_acc + contract_rows(activated, scaled_full)
        gain_acc = gain_acc + gain_term
        kept_terms = (
            lax.dynamic_update_slice_in_dim(kept_terms[0], normed_full, row_base + row_start, 0),
            lax.dynamic_update_slice_in_dim(kept_terms[1], grad_pre, row_base + row_start, 0),
        )
        return (out_rows, down_acc, gain_acc, kept_terms)

    out_rows, down_acc, gain_acc, kept_terms = lax.fori_loop(
        0, count_blocks, block_step, (out_rows,) + carried
    )
    return (out_rows, (down_acc, gain_acc, kept_terms))


def on_device(hidden_in, out_grad, pack_fill, norm_gain, up_weight, down_weight):
    weights = (norm_gain, up_weight, down_weight)
    shard_width = hidden_in.shape[2]
    ff_shard = up_weight.shape[1]
    model_width = up_weight.shape[0]
    down_acc = jnp.zeros((ff_shard, model_width), jnp.float32)
    gain_acc = jnp.zeros((shard_width,), jnp.float32)
    kept_terms = (
        jnp.zeros((MICRO * TOK_DEV, model_width), jnp.bfloat16),
        jnp.zeros((MICRO * TOK_DEV, ff_shard), jnp.bfloat16),
    )
    carried = (down_acc, gain_acc, kept_terms)
    results = []
    token_total = lax.psum(jnp.sum(pack_fill), "dp")
    inv_count = 1.0 / jnp.asarray(token_total).astype(jnp.float32)
    for micro_index in range(MICRO):
        out_rows, carried = run_rows(
            hidden_in[micro_index],
            out_grad[micro_index],
            pack_fill[micro_index, 0],
            TOK_DEV // BLOCK,
            inv_count,
            weights,
            carried,
            micro_index * TOK_DEV,
        )
        results.append(out_rows)
    in_grad = jnp.stack(results)
    down_acc, gain_acc, kept_terms = carried
    kept_normed, kept_pre = kept_terms
    up_grad = lax.psum_scatter(
        contract_rows(kept_normed, kept_pre).astype(jnp.bfloat16),
        "dp",
        scatter_dimension=0,
        tiled=True,
    ).astype(jnp.float32)
    down_grad = lax.psum_scatter(
        down_acc.astype(jnp.bfloat16), "dp", scatter_dimension=1, tiled=True
    ).astype(jnp.float32)
    gain_grad = lax.psum(gain_acc, "dp")
    return (in_grad, up_grad, down_grad, gain_grad)


def solution(mesh):
    in_specs = (
        P(None, "dp", "mp"),
        P(None, "dp", "mp"),
        P(None, "dp"),
        P("mp"),
        P(None, "mp"),
        P("mp", None),
    )
    out_specs = (P(None, "dp", "mp"), P("dp", "mp"), P("mp", "dp"), P("mp"))
    return jax.shard_map(
        on_device, mesh=mesh, in_specs=in_specs, out_specs=out_specs, check_vma=False
    )
```

profile of v0, /device:TPU:0, one launch (start us, length us, event | category | flops | bytes accessed | tf_op | source)
XLA Modules:
  0.0 585.8 jit_solution(11041027023317432150)
XLA Ops:
  7.2 0.0 reduce-scatter.15.cloned.1.call-start
  7.2 1.3 reduce_sum.69
  8.5 1.3 fusion.68
  9.8 13.7 %psum.46 = s32[]{:T(128)} all-reduce(s32[]{:T(128)} %reduce_sum.69), channel_id=1, replica_groups=mesh['dp'=8,'mp'=4] {'dp'}, use_global_device_ids=true, to_apply=%region_1.0 | all-reduce | flops 1 | bytes 8 | tf_op jit(solution)/shard_map/psum | solution.py:103
  24.2 1.2 fusion.29
  25.4 5.7 all-reduce.1
  31.1 1.2 fusion.31
  32.3 10.0 %all_gather.19 = bf16[128,3584]{1,0:T(8,128)(2,1)} all-gather(bf16[128,896]{1,0:T(8,128)(2,1)S(1)} %get-tuple-element.87), channel_id=1, replica_groups=mesh['dp'=8,'mp'=4] {'mp'}, dimensions={1}, use_global_device_ids=true | all-gather | bytes 1146880 | tf_op jit(solution)/shard_map/while/body/eval_jaxpr/all_gather | solution.py:39
  42.4 0.0 copy-start
  42.4 0.0 copy-start.4
  42.4 1.8 compare_convert_fusion
  44.2 2.0 fusion.48
  46.2 9.6 %all_gather.18 = bf16[128,3584]{1,0:T(8,128)(2,1)S(1)} all-gather(bf16[128,896]{1,0:T(8,128)(2,1)S(1)} %get-tuple-element.89), channel_id=1, replica_groups=mesh['dp'=8,'mp'=4] {'mp'}, dimensions={1}, use_global_device_ids=true | all-gather | bytes 1146880 | tf_op jit(solution)/shard_map/while/body/eval_jaxpr/all_gather | solution.py:40
  55.8 9.7 %fusion.70 = f32[128,1792]{1,0:T(8,128)} fusion(bf16[128,3584]{1,0:T(8,128)(2,1)S(1)} %all_gather.18, bf16[1792,3584]{1,0:T(8,128)(2,1)} %param.11), kind=kOutput, calls=%fused_computation.101 | convolution fusion | flops 1644167168 | bytes 14680064 | tf_op jit(solution)/shard_map/while/body/eval_jaxpr/dot_general | solution.py:25
  65.4 0.0 copy-done
  65.4 0.0 copy-done.4
  65.4 4.6 fusion.16
  70.0 6.2 %convolution_convert_fusion.1 = bf16[128,3584]{1,0:T(8,128)(2,1)} fusion(bf16[128,1792]{1,0:T(8,128)(2,1)} %get-tuple-element.112, bf16[3584,1792]{1,0:T(8,128)(2,1)S(1)} %copy-done), kind=kOutput, calls=%fused_computation.2 | convolution fusion | flops 1644625920 | bytes 14221312 | tf_op jit(solution)/shard_map/while/body/eval_jaxpr/dot_general | solution.py:25
  76.2 2.2 copy.12
  78.4 0.0 reduce-scatter.15.cloned.1.call-update
  78.5 0.0 reduce-scatter.13.cloned.1.call-start
  78.5 9.4 %all_gather.16 = bf16[128,3584]{1,0:T(8,128)(2,1)S(1)} all-gather(bf16[128,896]{1,0:T(8,128)(2,1)S(1)} %get-tuple-element.88), channel_id=1, replica_groups=mesh['dp'=8,'mp'=4] {'mp'}, dimensions={1}, use_global_device_ids=true | all-gather | bytes 1146880 | tf_op jit(solution)/shard_map/while/body/eval_jaxpr/all_gather | solution.py:40
  87.9 0.0 copy-start.1
  87.9 10.2 %fusion.69 = f32[128,1792]{1,0:T(8,128)} fusion(bf16[128,3584]{1,0:T(8,128)(2,1)S(1)} %all_gather.16, bf16[1792,3584]{1,0:T(8,128)(2,1)} %param.11), kind=kOutput, calls=%fused_computation.100 | convolution fusion | flops 1644167168 | bytes 14680064 | tf_op jit(solution)/shard_map/while/body/eval_jaxpr/dot_general | solution.py:25
  98.1 0.0 slice-start
  98.1 9.7 %all_gather.17 = bf16[128,3584]{1,0:T(8,128)(2,1)S(1)} all-gather(bf16[128,896]{1,0:T(8,128)(2,1)S(1)} %get-tuple-element.86), channel_id=1, replica_groups=mesh['dp'=8,'mp'=4] {'mp'}, dimensions={1}, use_global_device_ids=true | all-gather | bytes 1146880 | tf_op jit(solution)/shard_map/while/body/eval_jaxpr/all_gather | solution.py:39
  107.8 0.9 copy-done.5
  108.8 0.0 slice-start.1
  108.8 0.0 slice-start.2
  108.8 0.0 slice-start.3
  108.8 8.4 %fusion.9 = (bf16[128,1792]{1,0:T(8,128)(2,1)}, f32[128,1792]{1,0:T(8,128)}) fusion(f32[128,1792]{1,0:T(8,128)} %fusion.69, bf16[128,3584]{1,0:T(8,128)(2,1)S(1)} %all_gather.17, bf16[3584,1792]{1,0:T(8,128)(2,1)} %param.10), kind=kOutput, calls=%fused_computation.17 | convolution fusion | flops 1648754688 | bytes 16056320 | tf_op jit(solution)/shard_map/while/body/eval_jaxpr/dot_general | solution.py:42
  117.1 0.0 copy-done.1
  117.1 0.0 slice-done
  117.1 0.0 slice-done.1
  117.1 0.0 slice-done.2
  117.1 0.0 slice-done.3
  117.2 6.2 %convolution_convert_fusion.2 = bf16[128,3584]{1,0:T(8,128)(2,1)} fusion(bf16[128,1792]{1,0:T(8,128)(2,1)} %get-tuple-element.96, bf16[3584,1792]{1,0:T(8,128)(2,1)S(1)} %bitcast.45), kind=kOutput, calls=%fused_computation.3 | convolution fusion | flops 1644625920 | bytes 14221312 | tf_op jit(solution)/shard_map/while/body/eval_jaxpr/dot_general | solution.py:25
  123.3 2.2 copy.10
  125.6 0.0 reduce-scatter.13.cloned.1.call-update
  125.6 0.0 copy-start.2
  125.6 0.0 reduce-scatter.9.cloned.1.call-start
  125.7 10.0 %convolution_convert_fusion = bf16[3584,1792]{1,0:T(8,128)(2,1)} fusion(bf16[128,3584]{1,0:T(8,128)(2,1)} %all_gather.19, bf16[128,3584]{1,0:T(8,128)(2,1)} %copy-done.5, bf16[128,1792]{1,0:T(8,128)(2,1)} %get-tuple-element.112, bf16[128,1792]{1,0:T(8,128)(2,1)} %get-tuple-element.96), kind=kOutput, calls=%fused_computation.1 | convolution fusion | flops 3300261888 | bytes 15597568 | tf_op jit(solution)/shard_map/dot_general | solution.py:19
  135.7 0.0 reduce-scatter.9.cloned.1.call-update
  135.7 0.3 reduce-scatter.11.cloned.1.call-start
  136.0 0.0 copy-done.2
  136.0 11.6 %fusion.28 = f32[1792,3584]{0,1:T(8,128)} fusion(bf16[128,3584]{1,0:T(8,128)(2,1)S(1)} %copy-done.2, f32[128,1792]{1,0:T(8,128)} %get-tuple-element.97), kind=kOutput, calls=%fused_computation.50 | convolution fusion | flops 1646231552 | bytes 27525120 | tf_op jit(solution)/shard_map/while/body/eval_jaxpr/dot_general | solution.py:19
  147.6 15.3 %add_convert_fusion = bf16[1792,3584]{0,1:T(8,128)(2,1)} fusion(f32[1792,3584]{0,1:T(8,128)} %fusion.28, bf16[128,3584]{1,0:T(8,128)(2,1)S(1)} %all_gather.18, f32[128,1792]{1,0:T(8,128)} %get-tuple-element.113), kind=kOutput, calls=%fused_computation | convolution fusion | flops 1659076608 | bytes 40370176 | tf_op jit(solution)/shard_map/while/body/eval_jaxpr/dot_general | solution.py:19
  162.9 0.0 copy-start.3
  162.9 0.0 reduce-scatter.11.cloned.1.call-update
  162.9 0.0 reduce-scatter.15.cloned.1.call-done
  162.9 1.1 copy.13
  164.0 0.0 reduce-scatter.13.cloned.1.call-done
  164.1 1.1 copy.11
  165.2 0.0 copy-done.3
  165.2 0.0 copy-done.6
  165.2 0.4 fusion.36
  165.6 6.7 %all-reduce = (f32[128]{0:T(128)S(1)}, f32[128]{0:T(128)S(1)}) all-reduce(f32[128]{0:T(128)S(1)} %get-tuple-element.62, f32[128]{0:T(128)S(1)} %get-tuple-element.61), channel_id=1, replica_groups=mesh['dp'=8,'mp'=4] {'mp'}, use_global_device_ids=true, to_apply=%region_11.12 | all-reduce | flops 256 | bytes 2048 | tf_op jit(solution)/shard_map/while/body/eval_jaxpr/psum | solution.py:52
  172.4 20.8 %psum.51 = f32[896]{0:T(1024)} all-reduce(f32[896]{0:T(1024)S(1)} %add.104), channel_id=1, replica_groups=mesh['dp'=8,'mp'=4] {'dp'}, use_global_device_ids=true, to_apply=%region_16.17 | all-reduce | flops 896 | bytes 7168 | tf_op jit(solution)/shard_map/psum | solution.py:129
  193.2 0.4 fusion.57
  193.6 0.8 pad_maximum_fusion
  194.4 167.8 %reduce-scatter.9.cloned.1.call-done = bf16[448,1792]{1,0:T(8,128)(2,1)} async-done(((bf16[3584,1792]{1,0:T(8,128)(2,1)}), bf16[448,1792]{1,0:T(8,128)(2,1)}) %reduce-scatter.9.cloned.1.call-update) | async-done | bytes 1605648 | tf_op jit(solution)/shard_map/reduce_scatter | solution.py:120
  362.2 3.3 convert_element_type.149
  365.5 210.4 %reduce-scatter.11.cloned.1.call-done = bf16[1792,448]{0,1:T(8,128)(2,1)} async-done(((bf16[1792,3584]{0,1:T(8,128)(2,1)}), bf16[1792,448]{0,1:T(8,128)(2,1)}) %reduce-scatter.11.cloned.1.call-update) | async-done | bytes 1605648 | tf_op jit(solution)/shard_map/reduce_scatter | solution.py:126
  575.9 3.3 convert_element_type.153
  (5 shorter events, 0.0 us)
Async XLA Ops:
  7.2 155.7 %reduce-scatter.15.cloned.1.call-start = ((), (), s32[]{:S(2)}) async-start(), calls=%async_computation.7 | async-start | bytes 1146880
  42.4 23.1 %copy-start = (bf16[3584,1792]{1,0:T(8,128)(2,1)S(1)}, bf16[3584,1792]{1,0:T(8,128)(2,1)}, u32[]{:S(2)}) copy-start(bf16[3584,1792]{1,0:T(8,128)(2,1)} %param.10) | copy-start | bytes 38535172
  42.4 23.1 %copy-start.4 = (bf16[128,3584]{1,0:T(8,128)(2,1)S(1)}, bf16[128,3584]{1,0:T(8,128)(2,1)}, u32[]{:S(2)}) copy-start(bf16[128,3584]{1,0:T(8,128)(2,1)} %all_gather.19) | copy-start | bytes 2752516
  78.5 85.6 %reduce-scatter.13.cloned.1.call-start = ((), (), s32[]{:S(2)}) async-start(), calls=%async_computation.6 | async-start | bytes 1146880
  87.9 29.2 %copy-start.1 = (bf16[128,3584]{1,0:T(8,128)(2,1)}, bf16[128,3584]{1,0:T(8,128)(2,1)S(1)}, u32[]{:S(2)}) copy-start(bf16[128,3584]{1,0:T(8,128)(2,1)S(1)} %all_gather.16) | copy-start | bytes 2752516
  98.1 19.0 %slice-start = ((s8[12845056]{0:T(1024)(128)(4,1)}), s8[4194304]{0:T(1024)(128)(4,1)S(1)}, s32[]{:S(2)}) async-start(s8[12845056]{0:T(1024)(128)(4,1)} %bitcast.44), calls=%async_computation.8 | async-start | bytes 8388608
  107.8 0.9 copy-start.5
  108.8 8.4 %slice-start.1 = ((s8[12845056]{0:T(1024)(128)(4,1)}), s8[4194304]{0:T(1024)(128)(4,1)S(1)}, s32[]{:S(2)}) async-start(s8[12845056]{0:T(1024)(128)(4,1)} %bitcast.44), calls=%async_computation.9 | async-start | bytes 8388608
  108.8 8.4 %slice-start.2 = ((s8[12845056]{0:T(1024)(128)(4,1)}), s8[4194304]{0:T(1024)(128)(4,1)S(1)}, s32[]{:S(2)}) async-start(s8[12845056]{0:T(1024)(128)(4,1)} %bitcast.44), calls=%async_computation.10 | async-start | bytes 8388608
  108.8 8.4 %slice-start.3 = ((s8[12845056]{0:T(1024)(128)(4,1)}), s8[262144]{0:T(1024)(128)(4,1)S(1)}, s32[]{:S(2)}) async-start(s8[12845056]{0:T(1024)(128)(4,1)} %bitcast.44), calls=%async_computation.11 | async-start | bytes 524288
  125.6 10.4 %copy-start.2 = (bf16[128,3584]{1,0:T(8,128)(2,1)S(1)}, bf16[128,3584]{1,0:T(8,128)(2,1)}, u32[]{:S(2)}) copy-start(bf16[128,3584]{1,0:T(8,128)(2,1)} %copy-done.1) | copy-start | bytes 2752516
  125.6 236.6 %reduce-scatter.9.cloned.1.call-start = ((), (), s32[]{:S(2)}) async-start(), calls=%async_computation.4 | async-start | bytes 14450688 | tf_op jit(solution)/shard_map/reduce_scatter | solution.py:120
  135.7 440.2 %reduce-scatter.11.cloned.1.call-start = ((), (), s32[]{:S(2)}) async-start(), calls=%async_computation.5 | async-start | bytes 14450688 | tf_op jit(solution)/shard_map/reduce_scatter | solution.py:126
  162.9 2.3 copy-start.3
  162.9 2.3 copy-start.6
Sparse Core Ops, SparseCore 0:
  78.6 21.6 reduce-scatter.14
  125.7 21.4 reduce-scatter.12
  150.8 211.3 reduce-scatter.8
  365.7 210.2 reduce-scatter.10
where the time goes:
time: 586 us
  waiting for transfers between devices  378 us (65%)
  blocking collectives  85.6 us (15%)
  matrix products  82.1 us (14%)
  other arithmetic  15.8 us (3%)
  between operations  14.6 us (2%)
  local copies, waits for them, and re-layouts  8.97 us (2%)
    reduce_scatter x1, waiting for transfers between devices, on_device(): lax.psum_scatter(down_acc.astype(jnp.bfloat16), 'dp', scatter_dimension=1...  210 us
    reduce_scatter x1, waiting for transfers between devices, on_device(): lax.psum_scatter(contract_rows(kept_normed, kept_pre).astype(jnp.bfloat16...  168 us
    dot_general x3, matrix products, contract_rows(): lax.dot_general(left, right, (((0,), (0,)), ((), ())), preferred_element_...  36.9 us
    dot_general x4, matrix products, contract_cols(): lax.dot_general(left, right, (((1,), (1,)), ((), ())), preferred_element_...  32.2 us
    psum x1, blocking collectives, on_device(): gain_grad = lax.psum(gain_acc, 'dp')  20.8 us
    all_gather x2, blocking collectives, block_grads(): lax.all_gather(normed, 'mp', axis=1, tiled=True)  19.7 us
    all_gather x2, blocking collectives, block_grads(): lax.all_gather(scaled, 'mp', axis=1, tiled=True)  19 us
    psum x1, blocking collectives, on_device(): token_total = lax.psum(jnp.sum(pack_fill), 'dp')  13.7 us
  transfers between devices with their start and end apart: 4, of which 2 were waited for; matrix products, arithmetic and copies ran while one was open for 12% of the time, Pallas kernels for 0%

commit v1 on v0

v1 whole, which is shorter than its diff:
```python
import functools

import jax
import jax.numpy as jnp
from jax import lax
from jax.experimental import pallas as pl
from jax.experimental.pallas import tpu as pltpu
from jax.sharding import PartitionSpec as P


epsilon = 1e-06


def gelu_tanh(value):
    return jax.nn.gelu(value, approximate=True)


def contract_rows(left, right):
    return lax.dot_general(
        left, right, (((0,), (0,)), ((), ())), preferred_element_type=jnp.float32
    )


def contract_cols(left, right):
    return lax.dot_general(
        left, right, (((1,), (1,)), ((), ())), preferred_element_type=jnp.float32
    )


def stripe(rows, n_dp):
    micro, tok, width = rows.shape
    parts = []
    for m in range(micro):
        part = rows[m].reshape(tok // n_dp, n_dp, width).transpose(1, 0, 2)
        parts.append(part[::-1] if m % 2 else part)
    return jnp.concatenate(parts, axis=1)


def unstripe(slots, micro):
    n_dp, per, width = slots.shape
    share = per // micro
    outs = []
    for m in range(micro):
        part = slots[:, m * share : (m + 1) * share]
        part = part[::-1] if m % 2 else part
        outs.append(part.transpose(1, 0, 2).reshape(share * n_dp, width))
    return jnp.stack(outs)


def flipped(index, bit):
    return index + bit - 2 * bit * lax.rem(lax.div(index, bit), 2)


def flipped_by(index, mask):
    bit = 1
    while bit <= mask:
        if mask & bit:
            index = flipped(index, bit)
        bit *= 2
    return index


def exchange_kernel(axes, *refs):
    count = len(axes)
    ins, outs = refs[:count], refs[count : 2 * count]
    sems = refs[2 * count :]
    barrier = pltpu.get_barrier_semaphore()
    greeted = 0
    for axis in sorted({axis for axis, _ in axes}):
        n, me = lax.axis_size(axis), lax.axis_index(axis)
        for d in range(1, n):
            pl.semaphore_signal(
                barrier,
                inc=1,
                device_id={axis: lax.rem(me + d, n)},
                device_id_type=pl.DeviceIdType.MESH,
            )
        greeted += n - 1
    pl.semaphore_wait(barrier, greeted)

    def send(k, axis, source, target, peer, slot):
        copy = pltpu.make_async_remote_copy(
            src_ref=source,
            dst_ref=outs[k].at[target],
            send_sem=sems[2 * k].at[slot],
            recv_sem=sems[2 * k + 1].at[slot],
            device_id={axis: peer},
            device_id_type=pl.DeviceIdType.MESH,
        )
        copy.start()
        return copy

    trees = [k for k, (_, kind) in enumerate(axes) if kind == "tree"]
    copies = {}

    def forward(k, mask, below):
        axis = axes[k][0]
        me = lax.axis_index(axis)
        owner = flipped_by(me, mask)
        bit = below
        while bit >= 1:
            copies[k, mask ^ bit] = send(
                k,
                axis,
                outs[k].at[owner] if mask else ins[k],
                owner,
                flipped(me, bit),
                mask ^ bit,
            )
            bit //= 2

    for k in trees:
        forward(k, 0, lax.axis_size(axes[k][0]) // 2)
    locals_ = []
    for k, (axis, kind) in enumerate(axes):
        n, me = lax.axis_size(axis), lax.axis_index(axis)
        for d in [n // 2] + [d for d in range(1, n) if d != n // 2]:
            if kind == "tree":
                break
            peer = lax.rem(me + d, n)
            source = ins[k].at[peer] if kind == "split" else ins[k]
            copies[k, d] = send(k, axis, source, me, peer, d)
        own = pltpu.make_async_copy(
            ins[k].at[me] if kind == "split" else ins[k],
            outs[k].at[me],
            sems[2 * k].at[0],
        )
        own.start()
        locals_.append(own)
    relayed = set()
    if trees:
        n = lax.axis_size(axes[trees[0]][0])
        for mask in sorted(range(2, n, 2), key=lambda m: (bin(m).count("1"), -m)):
            for k in trees:
                copies[k, mask].wait_recv()
                relayed.add((k, mask))
                forward(k, mask, (mask & -mask) // 2)
    for key, copy in copies.items():
        copy.wait_send()
        if key not in relayed:
            copy.wait_recv()
    for own in locals_:
        own.wait()


def exchange(arrays, axes, collective_id):
    shapes, sems = [], []
    for array, (axis, kind) in zip(arrays, axes):
        n = lax.axis_size(axis)
        block = array.shape[1:] if kind == "split" else array.shape
        shapes.append(jax.ShapeDtypeStruct((n,) + block, array.dtype))
        sems += [pltpu.SemaphoreType.DMA((n,)), pltpu.SemaphoreType.DMA((n,))]
    vmem = pl.BlockSpec(memory_space=pltpu.VMEM)
    return pl.pallas_call(
        functools.partial(exchange_kernel, axes),
        out_shape=shapes,
        in_specs=[vmem] * len(arrays),
        out_specs=[vmem] * len(arrays),
        scratch_shapes=sems,
        compiler_params=pltpu.CompilerParams(
            collective_id=collective_id, has_side_effects=True
        ),
    )(*arrays)


def on_device(hidden_in, out_grad, pack_fill, norm_gain, up_weight, down_weight):
    micro, tok, width = hidden_in.shape
    model_width, ff_shard = up_weight.shape
    n_dp, n_mp = lax.axis_size("dp"), lax.axis_size("mp")
    me = lax.axis_index("dp")
    share = tok // n_dp
    slot_count = n_dp * micro * share
    chunk = -(-slot_count * 3 // 8 // 16) * 16
    cols = model_width // n_dp

    sent = stripe(jnp.concatenate([hidden_in, out_grad], axis=2), n_dp)
    fill_tile = jnp.broadcast_to(pack_fill, (micro, 128))
    gain_tile = jnp.broadcast_to(norm_gain[None, :], (8, width))
    slots, fills, gain_full = exchange(
        [sent, fill_tile, gain_tile],
        (("dp", "split"), ("dp", "all"), ("mp", "all")),
        0,
    )
    slots = slots.reshape(slot_count, 2 * width)
    fills = fills[:, :, 0].T
    gain_full = gain_full[:, 0, :].reshape(model_width)
    inv_count = 1.0 / jnp.sum(fills).astype(jnp.float32)

    odd = (jnp.arange(micro, dtype=jnp.int32) % 2)[None, :, None]
    steps = jnp.arange(share, dtype=jnp.int32)[None, None, :]
    start = jnp.where(odd == 1, n_dp - 1 - me, me)
    live = (start + steps * n_dp < fills.T[:, :, None]).reshape(slot_count)
    slot_ids = jnp.arange(slot_count, dtype=jnp.int32)
    before = (slot_ids[None, :] < slot_ids[:, None]) & live[None, :]
    place = jnp.where(live, jnp.sum(before.astype(jnp.int32), axis=1), -1)

    ranks = jnp.arange(n_dp, dtype=jnp.int32)[:, None, None]
    starts = jnp.where(odd.reshape(1, micro, 1) == 1, n_dp - 1 - ranks, ranks)
    counts = jnp.clip((fills[None] - starts + n_dp - 1) // n_dp, 0, share)
    most = jnp.max(jnp.sum(counts, axis=(1, 2)))
    chunk_total = (most + chunk - 1) // chunk

    def run_chunk(index):
        spots = jnp.arange(chunk, dtype=jnp.int32) + index * chunk
        pick = (spots[:, None] == place[None, :]).astype(jnp.bfloat16)
        packed = jnp.dot(pick, slots, preferred_element_type=jnp.float32)
        tok_rows = packed[:, :width].astype(jnp.bfloat16)
        scaled = (packed[:, width:] * inv_count).astype(jnp.bfloat16)
        (both,) = exchange(
            [jnp.concatenate([tok_rows, scaled], axis=1)], (("mp", "all"),), 1
        )
        both = both.transpose(1, 0, 2)
        tok_full = both[:, :, :width].reshape(chunk, model_width).astype(jnp.float32)
        scaled_full = both[:, :, width:].reshape(chunk, model_width)
        squares = jnp.sum(tok_full * tok_full, axis=1, keepdims=True)
        inv_rms = lax.rsqrt(squares / model_width + epsilon)
        normed_full = (tok_full * inv_rms * gain_full[None, :]).astype(jnp.bfloat16)
        pre_act = jnp.dot(normed_full, up_weight, preferred_element_type=jnp.float32)
        activated = gelu_tanh(pre_act).astype(jnp.bfloat16)
        grad_act = contract_cols(scaled_full, down_weight)
        grad_pre = jax.vjp(gelu_tanh, pre_act)[1](grad_act)[0].astype(jnp.bfloat16)

        by_cols = jnp.concatenate(
            [
                normed_full.reshape(chunk, n_dp, cols),
                scaled_full.reshape(chunk, n_dp, cols),
            ],
            axis=2,
        ).transpose(1, 0, 2)

        row_part = jnp.sum(grad_pre.astype(jnp.float32) * pre_act, axis=1, keepdims=True)
        partial = contract_cols(grad_pre, up_weight).astype(jnp.bfloat16)
        shares, row_parts = exchange(
            [
                partial.reshape(chunk, n_mp, width).transpose(1, 0, 2),
                jnp.broadcast_to(row_part / inv_rms, (chunk, 128)),
            ],
            (("mp", "split"), ("mp", "all")),
            2,
        )
        grad_normed = jnp.sum(shares.astype(jnp.float32), axis=0)
        row_dot = jnp.sum(row_parts, axis=0)[:, :1]
        values = tok_rows.astype(jnp.float32)
        cubed = inv_rms * inv_rms * inv_rms
        in_rows = (
            scaled.astype(jnp.float32)
            + norm_gain[None, :] * grad_normed * inv_rms
            - values * cubed * row_dot / model_width
        ).astype(jnp.bfloat16)
        gain_term = jnp.sum(grad_normed * values * inv_rms, axis=0)
        back = contract_rows(pick, in_rows).astype(jnp.bfloat16)
        act_all, pre_all, by_cols, back, gain_parts = exchange(
            [
                activated,
                grad_pre,
                by_cols,
                back.reshape(n_dp, micro * share, width),
                jnp.broadcast_to(gain_term[None, :], (8, width)),
            ],
            (("dp", "tree"), ("dp", "tree"), ("dp", "split"), ("dp", "split"), ("dp", "all")),
            3,
        )
        by_cols = by_cols.reshape(n_dp * chunk, 2 * cols)
        up_term = contract_rows(by_cols[:, :cols], pre_all.reshape(n_dp * chunk, ff_shard))
        down_term = contract_rows(act_all.reshape(n_dp * chunk, ff_shard), by_cols[:, cols:])
        return (back, up_term, down_term, jnp.sum(gain_parts[:, 0], axis=0))

    def add_chunk(index, total):
        return jax.tree.map(jnp.add, total, run_chunk(index))

    total = run_chunk(jnp.int32(0))
    back, up_grad, down_grad, gain_acc = lax.fori_loop(1, chunk_total, add_chunk, total)
    return (unstripe(back, micro), up_grad, down_grad, gain_acc)


def solution(mesh):
    in_specs = (
        P(None, "dp", "mp"),
        P(None, "dp", "mp"),
        P(None, "dp"),
        P("mp"),
        P(None, "mp"),
        P("mp", None),
    )
    out_specs = (P(None, "dp", "mp"), P("dp", "mp"), P("mp", "dp"), P("mp"))
    return jax.shard_map(
        on_device, mesh=mesh, in_specs=in_specs, out_specs=out_specs, check_vma=False
    )
```

time: 586 us -> 229 us (0.39)
  waiting for transfers between devices: 378 us -> 0 us
  Pallas kernels: 0 us -> 159 us
  blocking collectives: 85.6 us -> 0 us
  matrix products: 82.1 us -> 33.7 us
  between operations: 14.6 us -> 2.34 us
  local copies, waits for them, and re-layouts: 8.97 us -> 17.3 us
    reduce_scatter x2 -> x0, waiting for transfers between devices: 378 us -> none  [the longest x1 210 us: on_device(): lax.psum_scatter(down_acc.astype(jnp.bfloat16), 'dp', scatter_dimension=1...]
    pallas_call x0 -> x4, Pallas kernels: none -> 159 us  [exchange(): pl.pallas_call(functools.partial(exchange_kernel, axes), out_shape=shapes...]
    psum x4 -> x0, blocking collectives: 47 us -> none  [the longest x1 20.8 us: on_device(): gain_grad = lax.psum(gain_acc, 'dp')]
    all_gather x4 -> x0, blocking collectives: 38.7 us -> none  [the longest x2 19.7 us: block_grads(): lax.all_gather(normed, 'mp', axis=1, tiled=True)]
    dot_general x3, matrix products: 36.9 us -> 10.4 us  [contract_rows(): lax.dot_general(left, right, (((0,), (0,)), ((), ())), preferred_element_...]
    dot_general x4 -> x2, matrix products: 32.2 us -> 13.5 us  [contract_cols(): lax.dot_general(left, right, (((1,), (1,)), ((), ())), preferred_element_...]
    convert_element_type x5 -> x3, other arithmetic: 11.7 us -> 4.49 us  [the longest x1 2.68 us: run_chunk(): both[:, :, :width].reshape(chunk, model_width).astype(jnp.float32)]
  transfers between devices with their start and end apart: 4 -> 0, of which waited for: 2 -> 0; matrix products, arithmetic and copies ran while one was open for 12% -> 0% of each run, Pallas kernels for 0% -> 0%
where the time goes in v1:
time: 229 us; the launch traced here: 228 us
  Pallas kernels  159 us (69%)
  matrix products  33.7 us (15%)
  local copies, waits for them, and re-layouts  17.3 us (8%)
  other arithmetic  16 us (7%)
  between operations  2.34 us (1%)
    pallas_call x4, Pallas kernels, exchange(): pl.pallas_call(functools.partial(exchange_kernel, axes), out_shape=shapes...  159 us
    dot_general x2, matrix products, contract_cols(): lax.dot_general(left, right, (((1,), (1,)), ((), ())), preferred_element_...  13.5 us
    dot_general x3, matrix products, contract_rows(): lax.dot_general(left, right, (((0,), (0,)), ((), ())), preferred_element_...  10.4 us
    dot_general x1, matrix products, run_chunk(): jnp.dot(normed_full, up_weight, preferred_element_type=jnp.float32)  8.27 us

profile of v1, /device:TPU:0, one launch (start us, length us, event | category | flops | bytes accessed | tf_op | source)
XLA Modules:
  0.0 228.1 jit_solution(17288973773275399459)
XLA Ops:
  0.7 0.1 broadcast_add_fusion
  0.7 0.1 iota_select_fusion
  0.8 1.3 broadcast_in_dim.54.refs_1_
  2.1 1.3 broadcast_in_dim.55.refs_2_
  3.4 1.1 constant_dynamic-update-slice_fusion.1
  4.5 1.1 constant_dynamic-update-slice_fusion
  5.5 0.1 slice_bitcast_fusion.2
  5.6 0.2 copy_bitcast_fusion
  5.8 1.0 pad_maximum_fusion.1.refs_0_
  6.8 30.0 %shard_map.93 = (bf16[8,32,1792]{2,1,0:T(8,128)(2,1)}, s32[8,2,128]{2,1,0:T(2,128)}, f32[4,8,896]{2,1,0:T(8,128)}) custom-call(bf16[8,32,1792]{2,1,0:T(8,128)(2,1)} %pad_maximum_fusion.1.refs_0_, s32[2,128]{1,0:T(2,128)} %broadcast_in_dim.54.refs_1_, f32[8,896]{1,0:T(8,128)} %broadcast_in_dim.55.refs_2_), custom_call_target="tpu_custom_call" | custom-call | tf_op jit(solution)/shard_map/pallas_call | solution.py:154
  36.8 1.3 slice_reduce_fusion.4
  38.8 0.1 copy.87
  38.9 0.2 fusion.73
  39.1 0.6 reduce_max.9
  40.4 0.1 copy.88
  40.5 0.1 broadcast_compare_fusion
  40.6 0.1 lt.57
  40.7 0.1 convert_reduce_fusion.2
  40.8 0.6 broadcast_select_fusion
  41.4 0.9 fusion.81
  42.4 0.6 copy.96
  43.0 0.1 mul.444
  43.1 1.5 fusion.68
  44.6 0.9 copy-done.10
  45.4 0.8 pad_maximum_fusion.3.refs_0_
  46.2 19.3 %shard_map.94 = bf16[4,96,1792]{2,1,0:T(8,128)(2,1)} custom-call(bf16[96,1792]{1,0:T(8,128)(2,1)} %pad_maximum_fusion.3.refs_0_), custom_call_target="tpu_custom_call" | custom-call | tf_op jit(solution)/shard_map/pallas_call | solution.py:154
  65.5 1.3 multiply_reduce_fusion.2
  66.9 2.7 %slice_convert_fusion.2 = (f32[96,4,896]{2,0,1:T(8,128)S(1)}, bf16[4,12,8,896]{3,2,1,0:T(8,128)(2,1)}, f32[4,12,8,896]{3,2,1,0:T(8,128)S(1)}, bf16[96,4,896]{2,0,1:T(8,128)(2,1)}) fusion(bf16[96,4,1792]{2,0,1:T(8,128)(2,1)} %bitcast.138), kind=kLoop, calls=%fused_computation.88 | loop fusion | flops 344064 | bytes 5505024 | tf_op jit(solution)/shard_map/convert_element_type | solution.py:213
  69.5 2.0 copy.89
  71.5 1.9 reshape.302
  73.4 0.0 copy-start.17
  73.4 1.8 fusion.38
  75.2 0.1 copy.104
  75.3 9.6 %fusion.85 = f32[96,1792]{1,0:T(8,128)} fusion(bf16[96,3584]{1,0:T(8,128)(2,1)S(1)} %bitcast.141, bf16[1792,3584]{1,0:T(8,128)(2,1)} %param.13), kind=kOutput, calls=%fused_computation.163 | convolution fusion | flops 1233125376 | bytes 14221312 | tf_op jit(solution)/shard_map/dot_general | solution.py:25
  84.9 0.4 copy.90
  85.2 0.5 reshape_reshape.3
  85.7 0.0 copy-start.12
  85.7 0.2 copy.94
  86.0 0.9 copy-done.12
  86.9 1.5 maximum_bitcast_fusion.1.refs_2_
  88.4 0.1 copy.103
  88.5 0.0 copy-done.14
  88.5 0.0 slice-start.1
  88.6 0.0 slice-start.2
  88.6 0.0 slice-start.3
  88.6 8.3 %multiply_reduce_fusion.3 = (f32[96]{0:T(128)S(1)}, bf16[96,1792]{1,0:T(8,128)(2,1)S(1)}, bf16[96,1792]{1,0:T(8,128)(2,1)}) fusion(f32[96,1792]{1,0:T(8,128)S(1)} %copy-done.14, bf16[3584,1792]{1,0:T(8,128)(2,1)} %param.12, f32[96,3584]{1,0:T(8,128)S(1)} %bitcast.136, f32[3584]{0:T(1024)S(1)} %mul.425, f32[96]{0:T(128)S(1)} %fusion.77), kind=kOutput, calls=%fused_computation.89 | convolution fusion | flops 1238458240 | bytes 15612672 | tf_op jit(solution)/shard_map/dot_general | solution.py:218
  96.9 0.7 broadcast_in_dim.57.refs_1_
  97.6 0.0 slice-done.1
  97.6 0.0 slice-done.3
  97.6 4.0 %convolution_convert_fusion.2 = bf16[96,3584]{1,0:T(8,128)(2,1)S(1)} fusion(bf16[96,1792]{1,0:T(8,128)(2,1)S(1)} %get-tuple-element.296.refs_1_, bf16[3584,1792]{1,0:T(8,128)(2,1)S(1)} %bitcast.122), kind=kOutput, calls=%fused_computation.63 | convolution fusion | flops 1233469440 | bytes 13877248 | tf_op jit(solution)/shard_map/dot_general | solution.py:25
  101.6 0.0 copy-done.13
  101.6 0.9 copy.122
  102.5 14.1 %shard_map.95 = (bf16[4,96,896]{2,1,0:T(8,128)(2,1)}, f32[4,96,128]{2,1,0:T(8,128)}) custom-call(bf16[4,96,896]{2,1,0:T(8,128)(2,1)} %bitcast.140, f32[96,128]{1,0:T(8,128)} %broadcast_in_dim.57.refs_1_), custom_call_target="tpu_custom_call" | custom-call | tf_op jit(solution)/shard_map/pallas_call | solution.py:154
  116.6 1.3 convert_reduce_fusion.1
  117.9 0.1 fusion.59
  118.0 0.6 broadcast_in_dim.58.refs_4_
  118.7 0.1 slice_reduce_fusion.2
  118.8 1.9 convolution_convert_fusion.3
  120.7 95.3 %shard_map.96 = (bf16[8,96,1792]{2,1,0:T(8,128)(2,1)}, bf16[8,96,1792]{2,1,0:T(8,128)(2,1)}, bf16[8,96,896]{2,1,0:T(8,128)(2,1)}, bf16[8,32,896]{2,1,0:T(8,128)(2,1)}, f32[8,8,896]{2,1,0:T(8,128)}) custom-call(bf16[96,1792]{1,0:T(8,128)(2,1)} %get-tuple-element.310.refs_0_, bf16[96,1792]{1,0:T(8,128)(2,1)} %copy-done.13, ...), custom_call_target="tpu_custom_call" | custom-call | tf_op jit(solution)/shard_map/pallas_call | solution.py:154
  216.0 1.6 slice_reduce_fusion.3
  217.5 5.4 %fusion.39 = f32[1792,448]{0,1:T(8,128)} fusion(bf16[768,1792]{1,0:T(8,128)(2,1)} %bitcast.150, bf16[768,896]{1,0:T(8,128)(2,1)} %bitcast.146), kind=kOutput, calls=%fused_computation.75 | convolution fusion | flops 1233125376 | bytes 6750208 | tf_op jit(solution)/shard_map/dot_general | solution.py:19
  222.9 3.1 %fusion.41 = f32[448,1792]{1,0:T(8,128)} fusion(bf16[768,1792]{1,0:T(8,128)(2,1)S(1)} %bitcast.139, bf16[768,896]{1,0:T(8,128)(2,1)S(1)} %bitcast.147), kind=kOutput, calls=%fused_computation.77 | convolution fusion | flops 1233125376 | bytes 6750208 | tf_op jit(solution)/shard_map/dot_general | solution.py:19
  226.1 1.1 slice_bitcast_fusion.3
  227.3 0.8 pad_maximum_fusion.2
  (33 shorter events, 0.3 us)
Async XLA Ops:
  44.5 0.9 copy-start.10
  73.4 1.8 copy-start.17
  75.3 9.6 %copy-start.16 = (bf16[96,4,896]{2,0,1:T(8,128)(2,1)S(1)}, bf16[96,4,896]{2,0,1:T(8,128)(2,1)}, u32[]{:S(2)}) copy-start(bf16[96,4,896]{2,0,1:T(8,128)(2,1)} %get-tuple-element.307) | copy-start | bytes 2064388
  85.7 1.1 copy-start.12
  86.9 1.7 copy-start.14
  88.4 9.2 %slice-start = ((s8[12845056]{0:T(1024)(128)(4,1)}), s8[4194304]{0:T(1024)(128)(4,1)S(1)}, s32[]{:S(2)}) async-start(s8[12845056]{0:T(1024)(128)(4,1)} %bitcast.121), calls=%async_computation | async-start | bytes 8388608
  88.5 9.1 %slice-start.1 = ((s8[12845056]{0:T(1024)(128)(4,1)}), s8[4194304]{0:T(1024)(128)(4,1)S(1)}, s32[]{:S(2)}) async-start(s8[12845056]{0:T(1024)(128)(4,1)} %bitcast.121), calls=%async_computation.1 | async-start | bytes 8388608
  88.6 9.0 %slice-start.2 = ((s8[12845056]{0:T(1024)(128)(4,1)}), s8[4194304]{0:T(1024)(128)(4,1)S(1)}, s32[]{:S(2)}) async-start(s8[12845056]{0:T(1024)(128)(4,1)} %bitcast.121), calls=%async_computation.2 | async-start | bytes 8388608
  88.6 9.0 %slice-start.3 = ((s8[12845056]{0:T(1024)(128)(4,1)}), s8[262144]{0:T(1024)(128)(4,1)S(1)}, s32[]{:S(2)}) async-start(s8[12845056]{0:T(1024)(128)(4,1)} %bitcast.121), calls=%async_computation.3 | async-start | bytes 524288
  96.8 4.7 %copy-start.13 = (bf16[96,1792]{1,0:T(8,128)(2,1)}, bf16[96,1792]{1,0:T(8,128)(2,1)S(1)}, u32[]{:S(2)}) copy-start(bf16[96,1792]{1,0:T(8,128)(2,1)S(1)} %get-tuple-element.296.refs_1_) | copy-start | bytes 1032196
  101.6 16.3 %copy-start.11 = (f32[96,1792]{1,0:T(8,128)S(1)}, f32[96,1792]{1,0:T(8,128)}, u32[]{:S(2)}) copy-start(f32[96,1792]{1,0:T(8,128)} %copy-done.10) | copy-start | bytes 2064388
  116.6 2.0 copy-start.19
  217.5 5.4 %copy-start.15 = (bf16[8,96,1792]{2,1,0:T(8,128)(2,1)S(1)}, bf16[8,96,1792]{2,1,0:T(8,128)(2,1)}, u32[]{:S(2)}) copy-start(bf16[8,96,1792]{2,1,0:T(8,128)(2,1)} %get-tuple-element.195) | copy-start | bytes 8257540
  217.5 5.4 %copy-start.18 = (bf16[8,96,896]{2,1,0:T(8,128)(2,1)S(1)}, bf16[8,96,896]{2,1,0:T(8,128)(2,1)}, u32[]{:S(2)}) copy-start(bf16[8,96,896]{2,1,0:T(8,128)(2,1)} %get-tuple-element.194) | copy-start | bytes 4128772
